TPU v7x, 32 devices: a whole 2x2x4 slice. The times are simulated.
32 devices in a mesh: dp: 2 (over x), mp: 16 (over z, y, core).
Axes of the slice: x: 2, y: 2, z: 4, core: 2. Of those that a mesh axis runs over, the one named last changes fastest.
Arguments:
- grad_parts: bfloat16 [2, 16, 1, 512, 512], P('dp', 'mp'), may hold values from -0.1875 to 0.1875
- factors: float32 [16, 2, 512, 512], P('mp', 'dp'), may hold values from -1 to 8, as said below
- root_prev: bfloat16 [16, 2, 512, 512], P(None, 'dp', 'mp'), may hold values from -1 to 2, as said below
- plan: int32 [2, 16], P('dp'), may hold values from 0 to 16, as said below
Outputs:
- new_factors: float32 [16, 2, 512, 512], P('mp', 'dp')
- new_roots: bfloat16 [16, 2, 512, 512], P(None, 'dp', 'mp')
Inputs may be any that keep to these rules, and one draw needn't show every extreme that they name: In each row of plan no worker is named more than 3 times and one is named exactly 3 times; at least 8 entries of a row are below 16. `factors`: each factor is symmetric. `root_prev`: each root is symmetric.
All inputs are finite; a program needn't handle non-finite values.
Results may differ from a plain program's by a relative error of at most 0.0055.
Values may be sent and summed in bfloat16 or wider, within the bound.
A program may use at most 64 MiB of HBM per device.

v0:
```python
import functools

import jax
import jax.numpy as jnp
from jax import lax
from jax.experimental import pallas as pl
from jax.experimental.pallas import tpu as pltpu
from jax.sharding import PartitionSpec as P

keep_rate = 0.8
MESH = pl.DeviceIdType.MESH
F32 = jnp.float32
BF16 = jnp.bfloat16


def mul(a, b):
    return jnp.dot(a, b, preferred_element_type=F32)


def split(a):
    high = a.astype(BF16)
    return high, (a - high.astype(F32)).astype(BF16)


def kernel(
    n_dp, n_mp, blocks,
    plan, grad, fac, root, fresh, fac_out, plan_s,
    own_g, in_g, fac_v, root_v, pieces, full_x, rest, fifth, gram_v, out_v,
    load_sem, grad_send, grad_recv, root_send, root_recv, out_send, out_recv, turn,
):
    d = lax.axis_index("dp")
    me = lax.axis_index("mp")
    bs = fac.shape[-1]
    half = n_mp // 2
    hb = bs // 2
    side = me // half
    away = 1 - side
    near_cols = pl.ds(pl.multiple_of(side * hb, hb), hb)
    far_cols = pl.ds(pl.multiple_of(away * hb, hb), hb)
    near_pieces = pl.ds(side * half, half)
    far_pieces = pl.ds(away * half, half)

    def far_peer(i):
        return away * half + (me + i) % half

    def near_peer(i):
        return side * half + (me + i) % half

    loads = [
        pltpu.make_async_copy(grad, own_g, load_sem.at[0]),
        pltpu.make_async_copy(root, root_v, load_sem.at[1]),
        pltpu.make_async_copy(root.at[me], pieces.at[me], load_sem.at[2]),
        pltpu.make_async_copy(fac, fac_v, load_sem.at[3]),
        pltpu.make_async_copy(plan, plan_s, load_sem.at[4]),
    ]
    for load in loads:
        load.start()

    barrier = pltpu.get_barrier_semaphore()

    @pl.loop(1, n_mp)
    def _(i):
        pl.semaphore_signal(barrier, inc=1, device_id=(d, (me + i) % n_mp), device_id_type=MESH)

    for i in range(1, n_dp):
        pl.semaphore_signal(barrier, inc=1, device_id=((d + i) % n_dp, me), device_id_type=MESH)
    pl.semaphore_wait(barrier, n_mp - 1 + n_dp - 1)

    def grad_copy(i):
        other = (d + i) % n_dp
        return pltpu.make_async_remote_copy(
            src_ref=own_g.at[other * blocks // n_dp], dst_ref=in_g.at[i - 1],
            send_sem=grad_send.at[i - 1], recv_sem=grad_recv.at[i - 1],
            device_id=(other, me), device_id_type=MESH,
        )

    loads[0].wait()
    lead = me % 2 == 0

    @pl.when(lead)
    def _():
        for i in range(1, n_dp):
            grad_copy(i).start()

    def root_far(src, dst, peer, slot, cols):
        return pltpu.make_async_remote_copy(
            src_ref=root_v.at[src, :, cols], dst_ref=pieces.at[dst, :, cols],
            send_sem=root_send.at[peer], recv_sem=root_recv.at[slot],
            device_id=(d, peer), device_id_type=MESH,
        )

    def root_near(src, dst, peer, slot):
        return pltpu.make_async_remote_copy(
            src_ref=root_v.at[src], dst_ref=pieces.at[dst],
            send_sem=root_send.at[peer], recv_sem=root_recv.at[slot],
            device_id=(d, peer), device_id_type=MESH,
        )

    loads[1].wait()

    for parity in range(2):
        @pl.loop(0, half // 2)
        def _(i):
            t = away * half + (me // 2 * 2 + 2 * i) % half + parity
            root_far(t, me, t, me, near_cols).start()

        @pl.loop(0, half // 2)
        def _(i):
            t = side * half + (me // 2 * 2 + 2 * i) % half + parity

            @pl.when(t != me)
            def _():
                root_near(t, me, t, me).start()

    @pl.when(lead)
    def _():
        for i in range(1, n_dp):
            grad_copy(i).wait_send()
        pl.semaphore_signal(turn, inc=1, device_id=(d, me + 1), device_id_type=MESH)

    @pl.when(jnp.logical_not(lead))
    def _():
        pl.semaphore_wait(turn, 1)
        for i in range(1, n_dp):
            grad_copy(i).start()

    loads[2].wait()
    loads[3].wait()

    @pl.loop(0, half)
    def _(i):
        s = far_peer(i)
        root_far(s, s, s, s, far_cols).wait_recv()

    @pl.loop(1, half)
    def _(i):
        s = near_peer(i)
        root_near(s, s, s, s).wait_recv()

    near_rows = pieces[near_pieces].astype(F32).reshape(hb, bs).astype(BF16)
    full_x[near_cols, :] = near_rows
    full_x[far_cols, far_cols] = pieces[far_pieces, :, far_cols].astype(F32).reshape(hb, hb).astype(BF16)
    full_x[far_cols, near_cols] = full_x[near_cols, far_cols].astype(F32).T.astype(BF16)

    x = full_x[...]
    sq_h, sq_l = split(mul(x, x))
    fourth = (mul(sq_h, sq_h) + mul(sq_h, sq_l) + mul(sq_l, sq_h)).astype(BF16)
    fifth[...] = mul(x, fourth).astype(BF16)
    rest[...] = 1.25 * x.astype(F32) - (0.25 * keep_rate) * mul(fifth[...], fac_v[...].astype(BF16))

    for i in range(1, n_dp):
        grad_copy(i).wait_recv()
    total = own_g[d * blocks // n_dp].astype(F32)
    for i in range(1, n_dp):
        total += in_g[i - 1].astype(F32)
    summed = total.astype(BF16)

    @pl.when(d % 2 == 0)
    def _():
        gram_v[...] = lax.dot_general(summed, summed, (((1,), (1,)), ((), ())), preferred_element_type=F32)

    @pl.when(d % 2 == 1)
    def _():
        gram_v[...] = lax.dot_general(summed, summed, (((0,), (0,)), ((), ())), preferred_element_type=F32)

    gram_h = gram_v[...].astype(BF16)

    def out_copy(src, dst, peer, slot):
        return pltpu.make_async_remote_copy(
            src_ref=out_v.at[src], dst_ref=fresh.at[dst],
            send_sem=out_send.at[peer], recv_sem=out_recv.at[slot],
            device_id=(d, peer), device_id_type=MESH,
        )

    loads[4].wait()
    kept = plan_s[0, me] >= n_mp

    def refine(rows, at):
        refined = rest[rows, :] - (0.25 * (1.0 - keep_rate)) * mul(fifth[rows, :], gram_h)
        refined = jnp.where(kept, full_x[rows, :].astype(F32), refined)
        out_v[at] = refined.reshape(half, bs // n_mp, bs).astype(BF16)

    refine(far_cols, far_pieces)

    @pl.loop(0, half)
    def _(i):
        t = far_peer(i)
        out_copy(t, me, t, me).start()

    refine(near_cols, near_pieces)

    @pl.loop(1, half)
    def _(i):
        t = near_peer(i)
        out_copy(t, me, t, me).start()

    own_out = pltpu.make_async_copy(out_v.at[me], fresh.at[me], load_sem.at[0])
    own_out.start()
    fac_out[...] = keep_rate * fac_v[...] + (1.0 - keep_rate) * gram_v[...]

    @pl.when(jnp.logical_not(lead))
    def _():
        for i in range(1, n_dp):
            grad_copy(i).wait_send()

    @pl.loop(0, half)
    def _(i):
        t = far_peer(i)
        root_far(t, me, t, me, near_cols).wait_send()

    @pl.loop(1, half)
    def _(i):
        t = near_peer(i)
        root_near(t, me, t, me).wait_send()

    @pl.loop(1, n_mp)
    def _(i):
        s = (me + i) % n_mp
        out_copy(s, s, s, s).wait_send()
        out_copy(s, s, s, s).wait_recv()

    own_out.wait()


def local(n_dp, n_mp, grad_parts, factors, root_prev, plan):
    blocks, bs = grad_parts.shape[2], factors.shape[-1]
    rows = bs // n_mp
    grads = grad_parts.reshape(blocks, bs, bs)
    old = root_prev.reshape(n_mp, rows, bs)
    fresh, new_factor = pl.pallas_call(
        functools.partial(kernel, n_dp, n_mp, blocks),
        out_shape=(
            pltpu.VMEM((n_mp, rows, bs), BF16),
            pltpu.VMEM((bs, bs), F32),
        ),
        in_specs=[pl.BlockSpec(memory_space=pl.ANY)] * 4,
        out_specs=(pl.BlockSpec(memory_space=pltpu.VMEM),) * 2,
        scratch_shapes=[
            pltpu.SMEM(plan.shape, plan.dtype),
            pltpu.VMEM((blocks, bs, bs), BF16),
            pltpu.VMEM((n_dp - 1, bs, bs), BF16),
            pltpu.VMEM((bs, bs), F32),
            pltpu.VMEM((n_mp, rows, bs), BF16),
            pltpu.VMEM((n_mp, rows, bs), BF16),
            pltpu.VMEM((bs, bs), BF16),
            pltpu.VMEM((bs, bs), F32),
            pltpu.VMEM((bs, bs), BF16),
            pltpu.VMEM((bs, bs), F32),
            pltpu.VMEM((n_mp, rows, bs), BF16),
            pltpu.SemaphoreType.DMA((5,)),
            pltpu.SemaphoreType.DMA((n_dp - 1,)),
            pltpu.SemaphoreType.DMA((n_dp - 1,)),
            pltpu.SemaphoreType.DMA((n_mp,)),
            pltpu.SemaphoreType.DMA((n_mp,)),
            pltpu.SemaphoreType.DMA((n_mp,)),
            pltpu.SemaphoreType.DMA((n_mp,)),
            pltpu.SemaphoreType.REGULAR,
        ],
        compiler_params=pltpu.CompilerParams(collective_id=0, has_side_effects=True),
        name="refresh",
    )(plan, grads, factors.reshape(bs, bs), old)
    return (new_factor[None, None], fresh.reshape(root_prev.shape))


def solution(mesh):
    return jax.shard_map(
        functools.partial(local, mesh.shape["dp"], mesh.shape["mp"]),
        mesh=mesh,
        in_specs=(
            P("dp", "mp", None, None, None),
            P("mp", "dp", None, None),
            P(None, "dp", "mp", None),
            P("dp", None),
        ),
        out_specs=(P("mp", "dp", None, None), P(None, "dp", "mp", None)),
        check_vma=False,
    )
```

profile of v0, /device:TPU:0, one launch (start us, length us, event | category | flops | bytes accessed | tf_op | source)
XLA Modules:
  0.0 32.8 jit_solution(8550775660319924195)
XLA Ops:
  0.6 30.4 %refresh.1 = (bf16[16,32,512]{2,1,0:T(8,128)(2,1)S(1)}, f32[512,512]{1,0:T(8,128)S(1)}) custom-call(s32[1,16]{1,0:T(1,128)} %plan.1, bf16[1,512,512]{2,1,0:T(8,128)(2,1)} %bitcast.10, f32[512,512]{1,0:T(8,128)} %bitcast.9, bf16[16,32,512]{2,1,0:T(8,128)(2,1)} %bitcast.11), custom_call_target="tpu_custom_call" | custom-call | tf_op jit(solution)/shard_map/refresh/pallas_call | solution.py:230
  31.0 1.0 %copy.9 = f32[1,1,512,512]{3,2,1,0:T(8,128)} copy(f32[1,1,512,512]{3,2,1,0:T(8,128)S(1)} %bitcast.7) | data formatting | bytes 2097152
  32.0 0.8 %copy.10 = bf16[16,1,32,512]{3,2,1,0:T(8,128)(2,1)} copy(bf16[16,1,32,512]{3,2,1,0:T(8,128)(2,1)S(1)} %bitcast.8) | data formatting | bytes 1048576
where the time goes:
time: 32.9 us; the launch traced here: 32.8 us
  Pallas kernels  30.4 us (92%)
  local copies, waits for them, and re-layouts  1.77 us (5%)
  between operations  0.64 us (2%)
    pallas_call x1, Pallas kernels, local(): pl.pallas_call(functools.partial(kernel, n_dp, n_mp, blocks), out_shape=(...  30.4 us
    unnamed x2, local copies, waits for them, and re-layouts  1.77 us

commit v1 on v0

v1 whole, which is shorter than its diff:
```python
import functools

import jax
import jax.numpy as jnp
from jax import lax
from jax.experimental import pallas as pl
from jax.experimental.pallas import tpu as pltpu
from jax.sharding import PartitionSpec as P

keep_rate = 0.8
CHUNKS = 8
GROUP = 2
TURN = 5
MESH = pl.DeviceIdType.MESH
F32 = jnp.float32
BF16 = jnp.bfloat16


def mul(a, b):
    return jnp.dot(a, b, preferred_element_type=F32)


def scope(name):
    return jax.named_scope(name)


def kernel(
    n_dp, n_mp, blocks, row,
    plan, grad, fac, root, fresh, fac_out, plan_s,
    own_g, in_g, fac_v, root_v, pieces, full_x, rest, fifth, summed, gram_v, out_v,
    load_sem, grad_send, grad_recv, root_send, root_recv, out_send, out_recv, turn, above, below,
):
    d = lax.axis_index("dp")
    me = lax.axis_index("mp")
    bs = fac.shape[-1]
    half = n_mp // 2
    hb = bs // 2
    part = bs // CHUNKS
    wide = part * GROUP
    groups = CHUNKS // GROUP
    levels = n_mp // row
    level = me // row
    at = me % row
    side = me // half
    away = 1 - side
    near_cols = pl.ds(pl.multiple_of(side * hb, hb), hb)
    far_cols = pl.ds(pl.multiple_of(away * hb, hb), hb)
    far_first = pl.ds(pl.multiple_of(away * hb, hb), hb // 2)
    far_second = pl.ds(pl.multiple_of(away * hb + hb // 2, hb // 2), hb // 2)
    near_pieces = pl.ds(side * half, half)
    far_pieces = pl.ds(away * half, half)
    lead = me % 2 == 0
    has_above = level < levels - 1
    has_below = level > 0

    loads = [
        pltpu.make_async_copy(grad, own_g, load_sem.at[0]),
        pltpu.make_async_copy(root, root_v, load_sem.at[1]),
        pltpu.make_async_copy(root.at[me], pieces.at[me], load_sem.at[2]),
        pltpu.make_async_copy(fac, fac_v, load_sem.at[3]),
        pltpu.make_async_copy(plan, plan_s, load_sem.at[4]),
    ]

    def signal(sem, dp, mp):
        pl.semaphore_signal(sem, inc=1, device_id=(dp, mp), device_id_type=MESH)

    with scope("BARRIER"):
        barrier = pltpu.get_barrier_semaphore()
        for i in range(1, n_dp):
            signal(barrier, (d + i) % n_dp, me)
        for i in range(1, row):
            signal(barrier, d, level * row + (at + i) % row)

        @pl.when(has_below)
        def _():
            signal(barrier, d, me - row)

        @pl.when(has_above)
        def _():
            signal(barrier, d, me + row)

        for load in loads:
            load.start()
        pl.semaphore_wait(barrier, n_dp - 1 + row - 1 + has_below.astype(jnp.int32) + has_above.astype(jnp.int32))

        @pl.when(has_below)
        def _():
            signal(above.at[1], d, me - row)

        @pl.when(has_above)
        def _():
            signal(below.at[1], d, me + row)

        loads[0].wait()

    def grad_copy(i, c):
        other = (d + i) % n_dp
        rows = pl.ds(c * part, part)
        return pltpu.make_async_remote_copy(
            src_ref=own_g.at[other * blocks // n_dp, rows], dst_ref=in_g.at[i - 1, rows],
            send_sem=grad_send.at[i - 1, c], recv_sem=grad_recv.at[i - 1, c],
            device_id=(other, me), device_id_type=MESH,
        )

    grad_copies = [grad_copy(i, c) for c in range(CHUNKS) for i in range(1, n_dp)]

    @pl.when(lead)
    def _():
        for copy in grad_copies:
            copy.start()

    def root_far(src, dst, peer, slot, origin, act):
        base = origin // half * hb
        upper = origin % half < half // 2

        def copy(start, size):
            cols = pl.ds(pl.multiple_of(start, hb // 2), size)
            return pltpu.make_async_remote_copy(
                src_ref=root_v.at[src, :, cols], dst_ref=pieces.at[dst, :, cols],
                send_sem=root_send.at[peer], recv_sem=root_recv.at[slot],
                device_id=(d, peer), device_id_type=MESH,
            )

        @pl.when(upper)
        def _():
            act(copy(base, hb))

        @pl.when(jnp.logical_not(upper))
        def _():
            act(copy(base + hb // 2, hb // 2))

    def root_near(src, dst, peer, slot):
        return pltpu.make_async_remote_copy(
            src_ref=root_v.at[src], dst_ref=pieces.at[dst],
            send_sem=root_send.at[peer], recv_sem=root_recv.at[slot],
            device_id=(d, peer), device_id_type=MESH,
        )

    def send_roots(to, parity):
        for j in range(row // 2):
            t = to * row + (at // 2 * 2 + 2 * j) % row + parity
            close = t // half == side

            @pl.when(jnp.logical_not(close))
            def _():
                root_far(t, me, t, me, me, lambda copy: copy.start())

            @pl.when(jnp.logical_and(close, t != me))
            def _():
                root_near(t, me, t, me).start()

    def each_level(parity, meet):
        for k in range(1, levels):
            @pl.when(level + k < levels)
            def _():
                if meet:
                    pl.semaphore_wait(above.at[k], 1)
                    if k + 1 < levels:
                        @pl.when(has_below)
                        def _():
                            signal(above.at[k + 1], d, me - row)
                send_roots(level + k, parity)

            @pl.when(level >= k)
            def _():
                if meet:
                    pl.semaphore_wait(below.at[k], 1)
                    if k + 1 < levels:
                        @pl.when(has_above)
                        def _():
                            signal(below.at[k + 1], d, me + row)
                send_roots(level - k, parity)

        send_roots(level, parity)

    with scope("ROOTSEND"):
        loads[1].wait()
        each_level(0, True)

    with scope("TURN"):
        early = TURN * (n_dp - 1)

        @pl.when(lead)
        def _():
            for copy in grad_copies[:early]:
                copy.wait_send()
            signal(turn, d, me + 1)

        @pl.when(jnp.logical_not(lead))
        def _():
            pl.semaphore_wait(turn, 1)
            for copy in grad_copies:
                copy.start()

        each_level(1, False)

    def take_grad(c):
        rows = pl.ds(c * wide, wide)
        for j in range(GROUP):
            for i in range(1, n_dp):
                grad_copy(i, c * GROUP + j).wait_recv()
        total = own_g[d * blocks // n_dp, rows].astype(F32)
        for i in range(1, n_dp):
            total += in_g[i - 1, rows].astype(F32)
        s = total.astype(BF16)

        @pl.when(d % 2 == 0)
        def _():
            summed[rows, :] = s
            so_far = pl.ds(0, (c + 1) * wide)
            gram_v[rows, so_far] = lax.dot_general(s, summed[so_far, :], (((1,), (1,)), ((), ())), preferred_element_type=F32)
            if c:
                before = pl.ds(0, c * wide)
                gram_v[before, rows] = lax.dot_general(summed[before, :], s, (((1,), (1,)), ((), ())), preferred_element_type=F32)

        @pl.when(d % 2 == 1)
        def _():
            term = lax.dot_general(s, s, (((0,), (0,)), ((), ())), preferred_element_type=F32)
            gram_v[...] = term if c == 0 else gram_v[...] + term

    with scope("EARLYGRAD"):
        @pl.when(lead)
        def _():
            for c in range(groups - 1):
                take_grad(c)

    with scope("ROOTRECV"):
        loads[2].wait()
        loads[3].wait()

        @pl.loop(0, half)
        def _(i):
            s = away * half + i
            root_far(s, s, s, s, s, lambda copy: copy.wait_recv())

        @pl.loop(1, half)
        def _(i):
            s = side * half + (me + i) % half
            root_near(s, s, s, s).wait_recv()

    with scope("ASSEMBLE"):
        near_rows = pieces[near_pieces].astype(F32).reshape(hb, bs).astype(BF16)
        full_x[near_cols, :] = near_rows
        full_x[far_cols, far_cols] = pieces[far_pieces, :, far_cols].astype(F32).reshape(hb, hb).astype(BF16)
        full_x[far_second, far_first] = full_x[far_first, far_second].astype(F32).T.astype(BF16)
        full_x[far_cols, near_cols] = full_x[near_cols, far_cols].astype(F32).T.astype(BF16)

    with scope("CHAIN"):
        x = full_x[...]
        square = mul(x, x).astype(BF16)
        fourth = mul(square, square).astype(BF16)
        fifth[...] = mul(x, fourth).astype(BF16)
        rest[...] = 1.25 * x.astype(F32) - (0.25 * keep_rate) * mul(fifth[...], fac_v[...].astype(BF16))

    with scope("GRADS"):
        @pl.when(jnp.logical_not(lead))
        def _():
            for c in range(groups - 1):
                take_grad(c)
    with scope("GRADLAST"):
        take_grad(groups - 1)

    with scope("GRAMH"):
        gram_h = gram_v[...].astype(BF16)
        loads[4].wait()
        kept = plan_s[0, me] >= n_mp

    def out_copy(src, dst, peer, slot):
        return pltpu.make_async_remote_copy(
            src_ref=out_v.at[src], dst_ref=fresh.at[dst],
            send_sem=out_send.at[peer], recv_sem=out_recv.at[slot],
            device_id=(d, peer), device_id_type=MESH,
        )

    def refine(rows, to):
        refined = rest[rows, :] - (0.25 * (1.0 - keep_rate)) * mul(fifth[rows, :], gram_h)
        refined = jnp.where(kept, full_x[rows, :].astype(F32), refined)
        out_v[to] = refined.reshape(half, bs // n_mp, bs).astype(BF16)

    def send_out(t):
        out_copy(t, me, t, me).start()

    with scope("REF1"):
        refine(far_cols, far_pieces)

        @pl.loop(0, half // row)
        def _(k):
            for j in range(row):
                send_out(away * half + k * row + (at + j) % row)

    with scope("REF2"):
        refine(near_cols, near_pieces)

        @pl.loop(1, half)
        def _(i):
            send_out(side * half + (me + i) % half)

    with scope("FACOUT"):
        own_out = pltpu.make_async_copy(out_v.at[me], fresh.at[me], load_sem.at[0])
        own_out.start()
        fac_out[...] = keep_rate * fac_v[...] + (1.0 - keep_rate) * gram_v[...]

    with scope("SENDS"):
        @pl.when(lead)
        def _():
            for copy in grad_copies[early:]:
                copy.wait_send()

        @pl.when(jnp.logical_not(lead))
        def _():
            for copy in grad_copies:
                copy.wait_send()

        @pl.loop(0, half)
        def _(i):
            t = away * half + i
            root_far(t, me, t, me, me, lambda copy: copy.wait_send())

        @pl.loop(1, half)
        def _(i):
            t = side * half + (me + i) % half
            root_near(t, me, t, me).wait_send()

        @pl.loop(1, n_mp)
        def _(i):
            s = (me + i) % n_mp
            out_copy(s, s, s, s).wait_send()

        own_out.wait()

    with scope("RECVNEAR"):
        @pl.loop(1, half)
        def _(i):
            s = side * half + (me + i) % half
            out_copy(s, s, s, s).wait_recv()

    with scope("RECVFAR"):
        @pl.loop(0, half)
        def _(i):
            s = away * half + i
            out_copy(s, s, s, s).wait_recv()


def write_out(fac_v, fresh_v, fac_out, fresh_out, sem):
    n = 4
    copies = []
    for i in range(n):
        a = pl.ds(i * (fac_v.shape[0] // n), fac_v.shape[0] // n)
        b = pl.ds(i * (fresh_v.shape[0] // n), fresh_v.shape[0] // n)
        copies.append(pltpu.make_async_copy(fac_v.at[a], fac_out.at[a], sem.at[2 * i]))
        copies.append(pltpu.make_async_copy(fresh_v.at[b], fresh_out.at[b], sem.at[2 * i + 1]))
    for copy in copies:
        copy.start()
    for copy in copies:
        copy.wait()


def level_size(n_mp):
    size = 1
    while size * size < n_mp:
        size *= 2
    return size


def local(n_dp, n_mp, grad_parts, factors, root_prev, plan):
    blocks, bs = grad_parts.shape[2], factors.shape[-1]
    rows = bs // n_mp
    row = level_size(n_mp)
    grads = grad_parts.reshape(blocks, bs, bs)
    old = root_prev.reshape(n_mp, rows, bs)
    fresh, new_factor = pl.pallas_call(
        functools.partial(kernel, n_dp, n_mp, blocks, row),
        out_shape=(
            pltpu.VMEM((n_mp, rows, bs), BF16),
            pltpu.VMEM((bs, bs), F32),
        ),
        in_specs=[pl.BlockSpec(memory_space=pl.ANY)] * 4,
        out_specs=(pl.BlockSpec(memory_space=pltpu.VMEM),) * 2,
        scratch_shapes=[
            pltpu.SMEM(plan.shape, plan.dtype),
            pltpu.VMEM((blocks, bs, bs), BF16),
            pltpu.VMEM((n_dp - 1, bs, bs), BF16),
            pltpu.VMEM((bs, bs), F32),
            pltpu.VMEM((n_mp, rows, bs), BF16),
            pltpu.VMEM((n_mp, rows, bs), BF16),
            pltpu.VMEM((bs, bs), BF16),
            pltpu.VMEM((bs, bs), F32),
            pltpu.VMEM((bs, bs), BF16),
            pltpu.VMEM((bs, bs), BF16),
            pltpu.VMEM((bs, bs), F32),
            pltpu.VMEM((n_mp, rows, bs), BF16),
            pltpu.SemaphoreType.DMA((5,)),
            pltpu.SemaphoreType.DMA((n_dp - 1, CHUNKS)),
            pltpu.SemaphoreType.DMA((n_dp - 1, CHUNKS)),
            pltpu.SemaphoreType.DMA((n_mp,)),
            pltpu.SemaphoreType.DMA((n_mp,)),
            pltpu.SemaphoreType.DMA((n_mp,)),
            pltpu.SemaphoreType.DMA((n_mp,)),
            pltpu.SemaphoreType.REGULAR,
            pltpu.SemaphoreType.REGULAR((n_mp // row,)),
            pltpu.SemaphoreType.REGULAR((n_mp // row,)),
        ],
        compiler_params=pltpu.CompilerParams(collective_id=0, has_side_effects=True),
        name="refresh",
    )(plan, grads, factors.reshape(bs, bs), old)
    new_factor, fresh = pl.pallas_call(
        write_out,
        out_shape=(
            jax.ShapeDtypeStruct((bs, bs), F32),
            jax.ShapeDtypeStruct((n_mp, rows, bs), BF16),
        ),
        in_specs=[pl.BlockSpec(memory_space=pl.ANY)] * 2,
        out_specs=(pl.BlockSpec(memory_space=pl.ANY),) * 2,
        scratch_shapes=[pltpu.SemaphoreType.DMA((8,))],
        compiler_params=pltpu.CompilerParams(vmem_limit_bytes=1 << 20),
        name="write_out",
    )(new_factor, fresh)
    return (new_factor[None, None], fresh.reshape(root_prev.shape))


def solution(mesh):
    return jax.shard_map(
        functools.partial(local, mesh.shape["dp"], mesh.shape["mp"]),
        mesh=mesh,
        in_specs=(
            P("dp", "mp", None, None, None),
            P("mp", "dp", None, None),
            P(None, "dp", "mp", None),
            P("dp", None),
        ),
        out_specs=(P("mp", "dp", None, None), P(None, "dp", "mp", None)),
        check_vma=False,
    )
```

time: 32.9 us -> 30.3 us (0.921)
  the two profiles are of different devices: /device:TPU:0 before, /device:TPU:8 now
where the time goes in v1:
time: 30.3 us; the launch traced here: 29.7 us
  Pallas kernels  29.1 us (96%)
  between operations  0.64 us (2%)
    pallas_call x1, Pallas kernels, local(): pl.pallas_call(functools.partial(kernel, n_dp, n_mp, blocks, row), out_sh...  27.9 us
    pallas_call x1, Pallas kernels, local(): pl.pallas_call(write_out, out_shape=(jax.ShapeDtypeStruct((bs, bs), F32),...  1.2 us

profile of v1, /device:TPU:8, one launch (start us, length us, event | category | flops | bytes accessed | tf_op | source)
XLA Modules:
  0.0 29.7 jit_solution(12649943371047354204)
XLA Ops:
  0.6 27.9 %refresh.1 = (bf16[16,32,512]{2,1,0:T(8,128)(2,1)S(1)}, f32[512,512]{1,0:T(8,128)S(1)}) custom-call(s32[1,16]{1,0:T(1,128)} %plan.1, bf16[1,512,512]{2,1,0:T(8,128)(2,1)} %bitcast.8, f32[512,512]{1,0:T(8,128)} %bitcast.7, bf16[16,32,512]{2,1,0:T(8,128)(2,1)} %bitcast.9), custom_call_target="tpu_custom_call" | custom-call | tf_op jit(solution)/shard_map/refresh/pallas_call | solution.py:371
  28.5 1.2 %write_out.1 = (f32[512,512]{1,0:T(8,128)}, bf16[16,32,512]{2,1,0:T(8,128)(2,1)}) custom-call(f32[512,512]{1,0:T(8,128)S(1)} %get-tuple-element.6.fac_v, bf16[16,32,512]{2,1,0:T(8,128)(2,1)S(1)} %get-tuple-element.7.fresh_v), custom_call_target="tpu_custom_call" | custom-call | tf_op jit(solution)/shard_map/write_out/pallas_call | solution.py:406

commit v2 on v1

v2 whole, which is shorter than its diff:
```python
import functools

import jax
import jax.numpy as jnp
from jax import lax
from jax.experimental import pallas as pl
from jax.experimental.pallas import tpu as pltpu
from jax.sharding import PartitionSpec as P

keep_rate = 0.8
fresh_rate = 1.0 - keep_rate
GROUPS = 4
MESH = pl.DeviceIdType.MESH
F32 = jnp.float32
BF16 = jnp.bfloat16
scope = jax.named_scope


def mul(a, b, dims=(1, 0)):
    return lax.dot_general(a, b, (((dims[0],), (dims[1],)), ((), ())), preferred_element_type=F32)


def wait_bytes(ref, sem):
    pltpu.make_async_copy(ref, ref, sem).wait()


def kernel(
    n_dp, n_mp, blocks, row,
    plan, grad, fac, root, fresh, fac_out, plan_s,
    own_g, in_g, fac_v, pieces, full_x, rest, fifth, fac_b, summed, gram_b, out_v,
    load_sem, grad_send, grad_recv, gram_send, gram_recv, root_send, root_recv, out_send, out_recv, above,
):
    d = lax.axis_index("dp")
    me = lax.axis_index("mp")
    bs = fac.shape[-1]
    high = bs // n_mp
    half = n_mp // 2
    hb = bs // 2
    wide = bs // GROUPS
    levels = n_mp // row
    level = me // row
    at = me % row
    side = me // half
    away = 1 - side
    near_cols = pl.ds(pl.multiple_of(side * hb, hb), hb)
    far_cols = pl.ds(pl.multiple_of(away * hb, hb), hb)
    far_first = pl.ds(pl.multiple_of(away * hb, hb), hb // 2)
    far_second = pl.ds(pl.multiple_of(away * hb + hb // 2, hb // 2), hb // 2)
    near_pieces = pl.ds(side * half, half)
    far_pieces = pl.ds(away * half, half)
    parity = me % 2
    collects = d % 2 == parity
    partner = d + 1 - 2 * (d % 2)

    loads = [
        pltpu.make_async_copy(grad.at[d // 2], own_g, load_sem.at[0]),
        pltpu.make_async_copy(root.at[me], pieces.at[me], load_sem.at[1]),
        pltpu.make_async_copy(fac, fac_v, load_sem.at[2]),
        pltpu.make_async_copy(plan, plan_s, load_sem.at[3]),
    ]

    def signal(sem, dp, mp):
        pl.semaphore_signal(sem, inc=1, device_id=(dp, mp), device_id_type=MESH)

    def by_parity(act):
        @pl.when(parity == 0)
        def _():
            act(True)

        @pl.when(parity == 1)
        def _():
            act(False)

    with scope("BARRIER"):
        barrier = pltpu.get_barrier_semaphore()
        for i in range(1, n_dp):
            signal(barrier, (d + i) % n_dp, me)
        for i in range(1, row):
            signal(barrier, d, level * row + (at + i) % row)

        for k in range(1, levels):
            @pl.when(level + k < levels)
            def _():
                for i in range(row):
                    signal(barrier, d, (level + k) * row + (at + i) % row)

        for load in loads:
            load.start()
        pl.semaphore_wait(barrier, n_dp - 1 + row - 1 + level * row)

        for k in range(1, levels):
            @pl.when(level >= k)
            def _():
                signal(above.at[k], d, me - k * row)

    def strip(ref, c, by_cols):
        cut = pl.ds(c * wide, wide)
        return ref.at[:, cut] if by_cols else ref.at[cut, :]

    def send_grads(by_cols):
        for c in range(GROUPS):
            for k in range(blocks):
                to = 2 * k + parity

                @pl.when(to != d)
                def _():
                    pltpu.make_async_remote_copy(
                        src_ref=strip(grad.at[k], c, by_cols),
                        dst_ref=strip(in_g.at[(d - to + n_dp) % n_dp - 1], c, by_cols),
                        send_sem=grad_send.at[c // (GROUPS - 1)], recv_sem=grad_recv.at[c],
                        device_id=(to, me), device_id_type=MESH,
                    ).start()

    by_parity(send_grads)

    def root_far(t):
        base = side * hb
        upper = me % half < half // 2

        def copy(start, size):
            cols = pl.ds(pl.multiple_of(start, hb // 2), size)
            pltpu.make_async_remote_copy(
                src_ref=root.at[t, :, cols], dst_ref=pieces.at[me, :, cols],
                send_sem=root_send, recv_sem=root_recv, device_id=(d, t), device_id_type=MESH,
            ).start()

        @pl.when(upper)
        def _():
            copy(base, hb)

        @pl.when(jnp.logical_not(upper))
        def _():
            copy(base + hb // 2, hb // 2)

    def root_near(t):
        pltpu.make_async_remote_copy(
            src_ref=root.at[t], dst_ref=pieces.at[me],
            send_sem=root_send, recv_sem=root_recv, device_id=(d, t), device_id_type=MESH,
        ).start()

    def send_roots(to, odd):
        for j in range(row // 2):
            t = to * row + (at // 2 * 2 + 2 * j) % row + odd
            close = t // half == side

            @pl.when(jnp.logical_not(close))
            def _():
                root_far(t)

            @pl.when(jnp.logical_and(close, t != me))
            def _():
                root_near(t)

    def each_level(odd, meet):
        for k in reversed(range(1, levels)):
            @pl.when(level >= k)
            def _():
                send_roots(level - k, odd)

        send_roots(level, odd)

        for k in range(1, levels):
            @pl.when(level + k < levels)
            def _():
                if meet:
                    pl.semaphore_wait(above.at[k], 1)
                send_roots(level + k, odd)

    with scope("ROOTSEND"):
        each_level(d % 2, True)

    def take(c, by_cols):
        wait_bytes(in_g.at[:, :, pl.ds(c * wide, wide)] if by_cols else in_g.at[:, pl.ds(c * wide, wide), :], grad_recv.at[c])
        total = strip(own_g, c, by_cols)[...].astype(F32)
        for i in range(n_dp - 1):
            total += strip(in_g.at[i], c, by_cols)[...].astype(F32)
        strip(summed, c, by_cols)[...] = total.astype(BF16)

    def make_row(c, by_cols):
        new = strip(summed, c, by_cols)[...]
        so_far = pl.ds(0, (c + 1) * wide)
        product = mul(new, summed[:, so_far], (0, 0)) if by_cols else mul(new, summed[so_far, :], (1, 1))
        gram_b[pl.ds(c * wide, wide), so_far] = (fresh_rate * product).astype(BF16)

    def gram_row(c):
        part = gram_b.at[pl.ds(c * wide, wide), pl.ds(0, (c + 1) * wide)]
        return pltpu.make_async_remote_copy(
            src_ref=part, dst_ref=part, send_sem=gram_send.at[c], recv_sem=gram_recv.at[c],
            device_id=(partner, me), device_id_type=MESH,
        )

    early = GROUPS // 2
    loads[0].wait()

    with scope("EARLY"):
        @pl.when(collects)
        def _():
            def act(by_cols):
                for c in range(early):
                    take(c, by_cols)
                    make_row(c, by_cols)
                    if c == 0:
                        each_level(1 - d % 2, False)

            by_parity(act)

        @pl.when(jnp.logical_not(collects))
        def _():
            wait_bytes(in_g.at[pl.ds(0, blocks), pl.ds(0, bs - wide), :], grad_send.at[0])
            each_level(1 - d % 2, False)

    with scope("ROOTRECV"):
        loads[1].wait()
        loads[2].wait()
        wait_bytes(pieces.at[pl.ds(0, half - 1 + half * 3 // 8)], root_recv)

    loads[3].wait()
    kept = plan_s[0, me] >= n_mp
    x_rate = jnp.where(kept, 1.0, 1.25)
    step = jnp.where(kept, 0.0, 0.25)

    with scope("ASSEMBLE"):
        near_rows = pieces[near_pieces].astype(F32).reshape(hb, bs).astype(BF16)
        full_x[near_cols, :] = near_rows
        full_x[far_cols, far_cols] = pieces[far_pieces, :, far_cols].astype(F32).reshape(hb, hb).astype(BF16)
        full_x[far_second, far_first] = full_x[far_first, far_second].astype(F32).T.astype(BF16)
        full_x[far_cols, near_cols] = full_x[near_cols, far_cols].astype(F32).T.astype(BF16)

    with scope("CHAIN"):
        x = full_x[...]
        square = mul(x, x).astype(BF16)
        fourth = mul(square, square).astype(BF16)
        fifth[...] = (step * mul(x, fourth)).astype(BF16)

    def send_out(t):
        pltpu.make_async_remote_copy(
            src_ref=out_v.at[t], dst_ref=fresh.at[me],
            send_sem=out_send, recv_sem=out_recv, device_id=(d, t), device_id_type=MESH,
        ).start()

    def refine(first, count, base, factor):
        rows = pl.ds(pl.multiple_of(first * high, high), count * high)
        refined = base(rows) - mul(fifth[rows, :], factor[...])
        out_v[pl.ds(first, count)] = refined.reshape(count, high, bs).astype(BF16)

    def give_far(base, factor):
        for k in range(half // row):
            refine(away * half + k * row, row, base, factor)
            for j in range(row):
                send_out(away * half + k * row + j // 2 * 2 + (j + at) % 2)

    def give_near(base, factor):
        refine(side * half, half, base, factor)

        @pl.loop(1, half)
        def _(i):
            send_out(side * half + (me + i) % half)

    def part_x(rows):
        return x_rate * full_x[rows, :].astype(F32)

    @pl.when(collects)
    def _():
        def act(by_cols):
            dims = (1, 1) if by_cols else (0, 0)
            last = GROUPS - 1
            with scope("GRADS"):
                for c in range(early, last):
                    take(c, by_cols)
                    make_row(c, by_cols)
                for c in range(last):
                    gram_row(c).start()
                cut = pl.ds(0, last * wide)
                known = summed[:, cut] if by_cols else summed[cut, :]
                fac_out[...] = keep_rate * fac_v[...] + fresh_rate * mul(known, known, dims)
            with scope("GRADLAST"):
                take(last, by_cols)
                new = strip(summed, last, by_cols)[...]
                total = fac_out[...] + fresh_rate * mul(new, new, dims)
                fac_out[...] = total
                fac_b[...] = total.astype(BF16)
            with scope("GIVEFAR"):
                give_far(part_x, fac_b)
            with scope("ROWLAST"):
                make_row(last, by_cols)
                gram_row(last).start()
            with scope("GIVENEAR"):
                give_near(part_x, fac_b)
            for c in range(GROUPS):
                gram_row(c).wait_send()

        by_parity(act)

    @pl.when(jnp.logical_not(collects))
    def _():
        with scope("REST"):
            rest[...] = x_rate * full_x[...].astype(F32) - keep_rate * mul(fifth[...], fac_v[...].astype(BF16))
        for c in range(GROUPS):
            with scope("GRAMIN%d" % c):
                gram_row(c).wait_recv()
                if c:
                    rows = pl.ds(c * wide, wide)
                    before = pl.ds(0, c * wide)
                    gram_b[before, rows] = gram_b[rows, before].astype(F32).T.astype(BF16)
        with scope("GIVEFAR"):
            give_far(lambda rows: rest[rows, :], gram_b)
        with scope("GIVENEAR"):
            give_near(lambda rows: rest[rows, :], gram_b)
        with scope("FACOUT"):
            fac_out[...] = keep_rate * fac_v[...] + gram_b[...].astype(F32)
            wait_bytes(in_g.at[pl.ds(0, blocks), pl.ds(0, wide), :], grad_send.at[1])

    with scope("SENDS"):
        own_out = pltpu.make_async_copy(out_v.at[me], fresh.at[me], load_sem.at[0])
        own_out.start()
        if blocks > 1:
            @pl.when(collects)
            def _():
                wait_bytes(in_g.at[pl.ds(0, blocks - 1), pl.ds(0, bs - wide), :], grad_send.at[0])
                wait_bytes(in_g.at[pl.ds(0, blocks - 1), pl.ds(0, wide), :], grad_send.at[1])

        @pl.when(me % half < half // 2)
        def _():
            wait_bytes(pieces.at[pl.ds(0, half - 1 + half // 2)], root_send)

        @pl.when(me % half >= half // 2)
        def _():
            wait_bytes(pieces.at[pl.ds(0, half - 1 + half // 4)], root_send)

        own_out.wait()
        wait_bytes(out_v.at[pl.ds(0, n_mp - 1)], out_send)

    with scope("RECV"):
        wait_bytes(fresh.at[pl.ds(0, n_mp - 1)], out_recv)


def write_out(fac_v, fresh_v, fac_out, fresh_out, sem):
    n = 4
    copies = []
    for i in range(n):
        a = pl.ds(i * (fac_v.shape[0] // n), fac_v.shape[0] // n)
        b = pl.ds(i * (fresh_v.shape[0] // n), fresh_v.shape[0] // n)
        copies.append(pltpu.make_async_copy(fac_v.at[a], fac_out.at[a], sem.at[2 * i]))
        copies.append(pltpu.make_async_copy(fresh_v.at[b], fresh_out.at[b], sem.at[2 * i + 1]))
    for copy in copies:
        copy.start()
    for copy in copies:
        copy.wait()


def level_size(n_mp):
    size = 1
    while size * size < n_mp:
        size *= 2
    return size


def local(n_dp, n_mp, grad_parts, factors, root_prev, plan):
    blocks, bs = grad_parts.shape[2], factors.shape[-1]
    high = bs // n_mp
    row = level_size(n_mp)
    wide = bs // GROUPS
    grads = grad_parts.reshape(blocks, bs, bs)
    old = root_prev.reshape(n_mp, high, bs)
    fresh, new_factor = pl.pallas_call(
        functools.partial(kernel, n_dp, n_mp, blocks, row),
        out_shape=(
            pltpu.VMEM((n_mp, high, bs), BF16),
            pltpu.VMEM((bs, bs), F32),
        ),
        in_specs=[pl.BlockSpec(memory_space=pl.ANY)] * 4,
        out_specs=(pl.BlockSpec(memory_space=pltpu.VMEM),) * 2,
        scratch_shapes=[
            pltpu.SMEM(plan.shape, plan.dtype),
            pltpu.VMEM((bs, bs), BF16),
            pltpu.VMEM((n_dp - 1, bs, bs), BF16),
            pltpu.VMEM((bs, bs), F32),
            pltpu.VMEM((n_mp, high, bs), BF16),
            pltpu.VMEM((bs, bs), BF16),
            pltpu.VMEM((bs, bs), F32),
            pltpu.VMEM((bs, bs), BF16),
            pltpu.VMEM((bs, bs), BF16),
            pltpu.VMEM((bs, bs), BF16),
            pltpu.VMEM((bs, bs), BF16),
            pltpu.VMEM((n_mp, high, bs), BF16),
            pltpu.SemaphoreType.DMA((4,)),
            pltpu.SemaphoreType.DMA((2,)),
            pltpu.SemaphoreType.DMA((GROUPS,)),
            pltpu.SemaphoreType.DMA((GROUPS,)),
            pltpu.SemaphoreType.DMA((GROUPS,)),
            pltpu.SemaphoreType.DMA,
            pltpu.SemaphoreType.DMA,
            pltpu.SemaphoreType.DMA,
            pltpu.SemaphoreType.DMA,
            pltpu.SemaphoreType.REGULAR((n_mp // row,)),
        ],
        compiler_params=pltpu.CompilerParams(collective_id=0, has_side_effects=True),
        name="refresh",
    )(plan, grads, factors.reshape(bs, bs), old)
    new_factor, fresh = pl.pallas_call(
        write_out,
        out_shape=(
            jax.ShapeDtypeStruct((bs, bs), F32),
            jax.ShapeDtypeStruct((n_mp, high, bs), BF16),
        ),
        in_specs=[pl.BlockSpec(memory_space=pl.ANY)] * 2,
        out_specs=(pl.BlockSpec(memory_space=pl.ANY),) * 2,
        scratch_shapes=[pltpu.SemaphoreType.DMA((8,))],
        compiler_params=pltpu.CompilerParams(vmem_limit_bytes=1 << 20),
        name="write_out",
    )(new_factor, fresh)
    return (new_factor[None, None], fresh.reshape(root_prev.shape))


def solution(mesh):
    return jax.shard_map(
        functools.partial(local, mesh.shape["dp"], mesh.shape["mp"]),
        mesh=mesh,
        in_specs=(
            P("dp", "mp", None, None, None),
            P("mp", "dp", None, None),
            P(None, "dp", "mp", None),
            P("dp", None),
        ),
        out_specs=(P("mp", "dp", None, None), P(None, "dp", "mp", None)),
        check_vma=False,
    )
```

time: 30.3 us -> 27.5 us (0.908)
  the two profiles are of different devices: /device:TPU:8 before, /device:TPU:12 now
where the time goes in v2:
time: 27.5 us; the launch traced here: 27.4 us
  Pallas kernels  26.7 us (97%)
  between operations  0.64 us (2%)
    pallas_call x1, Pallas kernels, local(): pl.pallas_call(functools.partial(kernel, n_dp, n_mp, blocks, row), out_sh...  25.5 us
    pallas_call x1, Pallas kernels, local(): pl.pallas_call(write_out, out_shape=(jax.ShapeDtypeStruct((bs, bs), F32),...  1.2 us

profile of v2, /device:TPU:12, one launch (start us, length us, event | category | flops | bytes accessed | tf_op | source)
XLA Modules:
  0.0 27.4 jit_solution(2440861483674654615)
XLA Ops:
  0.6 25.5 %refresh.1 = (bf16[16,32,512]{2,1,0:T(8,128)(2,1)S(1)}, f32[512,512]{1,0:T(8,128)S(1)}) custom-call(s32[1,16]{1,0:T(1,128)} %plan.1, bf16[1,512,512]{2,1,0:T(8,128)(2,1)} %bitcast.8, f32[512,512]{1,0:T(8,128)} %bitcast.7, bf16[16,32,512]{2,1,0:T(8,128)(2,1)} %bitcast.9), custom_call_target="tpu_custom_call" | custom-call | tf_op jit(solution)/shard_map/refresh/pallas_call | solution.py:365
  26.2 1.2 %write_out.1 = (f32[512,512]{1,0:T(8,128)}, bf16[16,32,512]{2,1,0:T(8,128)(2,1)}) custom-call(f32[512,512]{1,0:T(8,128)S(1)} %get-tuple-element.6.fac_v, bf16[16,32,512]{2,1,0:T(8,128)(2,1)S(1)} %get-tuple-element.7.fresh_v), custom_call_target="tpu_custom_call" | custom-call | tf_op jit(solution)/shard_map/write_out/pallas_call | solution.py:400

commit v3 on v2

--- a/solution.py
+++ b/solution.py
@@ -40,6 +40,9 @@
     levels = n_mp // row
     level = me // row
     at = me % row
+    band = row // 2
+    upper_band = at >= band
+    start = me - at % band
     side = me // half
     away = 1 - side
     near_cols = pl.ds(pl.multiple_of(side * hb, hb), hb)
@@ -75,23 +78,35 @@
         barrier = pltpu.get_barrier_semaphore()
         for i in range(1, n_dp):
             signal(barrier, (d + i) % n_dp, me)
-        for i in range(1, row):
-            signal(barrier, d, level * row + (at + i) % row)
-
+        for i in range(1, band):
+            signal(barrier, d, start + (at + i) % band)
         for k in range(1, levels):
             @pl.when(level + k < levels)
             def _():
-                for i in range(row):
-                    signal(barrier, d, (level + k) * row + (at + i) % row)
+                for i in range(band):
+                    signal(barrier, d, start + k * row + (at + i) % band)
+
+        @pl.when(jnp.logical_not(upper_band))
+        def _():
+            for k in range(levels):
+                @pl.when(level + k < levels)
+                def _():
+                    for i in range(band):
+                        signal(barrier, d, start + k * row + band + (at + i) % band)
 
         for load in loads:
             load.start()
-        pl.semaphore_wait(barrier, n_dp - 1 + row - 1 + level * row)
-
-        for k in range(1, levels):
-            @pl.when(level >= k)
-            def _():
-                signal(above.at[k], d, me - k * row)
+        known = n_dp - 1 + band - 1 + level * band
+        pl.semaphore_wait(barrier, jnp.where(upper_band, known + (level + 1) * band, known))
+
+        @pl.when(upper_band)
+        def _():
+            for k in range(levels):
+                @pl.when(level >= k)
+                def _():
+                    signal(above.at[k], d, me - k * row - band)
+                    if k:
+                        signal(above.at[k], d, me - k * row)
 
     def strip(ref, c, by_cols):
         cut = pl.ds(c * wide, wide)
@@ -139,8 +154,8 @@
         ).start()
 
     def send_roots(to, odd):
-        for j in range(row // 2):
-            t = to * row + (at // 2 * 2 + 2 * j) % row + odd
+        for j in range(band // 2):
+            t = to + (at // 2 * 2 + 2 * j) % band + odd
             close = t // half == side
 
             @pl.when(jnp.logical_not(close))
@@ -152,19 +167,28 @@
                 root_near(t)
 
     def each_level(odd, meet):
-        for k in reversed(range(1, levels)):
+        for k in reversed(range(levels)):
             @pl.when(level >= k)
             def _():
-                send_roots(level - k, odd)
-
-        send_roots(level, odd)
+                send_roots((level - k) * row, odd)
+
+        if meet:
+            @pl.when(jnp.logical_not(upper_band))
+            def _():
+                pl.semaphore_wait(above.at[0], 1)
+
+        for k in reversed(range(levels)):
+            @pl.when(level >= k)
+            def _():
+                send_roots((level - k) * row + band, odd)
 
         for k in range(1, levels):
             @pl.when(level + k < levels)
             def _():
                 if meet:
                     pl.semaphore_wait(above.at[k], 1)
-                send_roots(level + k, odd)
+                send_roots((level + k) * row, odd)
+                send_roots((level + k) * row + band, odd)
 
     with scope("ROOTSEND"):
         each_level(d % 2, True)
@@ -267,8 +291,7 @@
             with scope("GRADS"):
                 for c in range(early, last):
                     take(c, by_cols)
-                    make_row(c, by_cols)
-                for c in range(last):
+                for c in range(early):
                     gram_row(c).start()
                 cut = pl.ds(0, last * wide)
                 known = summed[:, cut] if by_cols else summed[cut, :]
@@ -276,16 +299,17 @@
             with scope("GRADLAST"):
                 take(last, by_cols)
                 new = strip(summed, last, by_cols)[...]
-                total = fac_out[...] + fresh_rate * mul(new, new, dims)
-                fac_out[...] = total
-                fac_b[...] = total.astype(BF16)
+                fac_b[...] = (fac_out[...] + fresh_rate * mul(new, new, dims)).astype(BF16)
             with scope("GIVEFAR"):
                 give_far(part_x, fac_b)
             with scope("ROWLAST"):
-                make_row(last, by_cols)
-                gram_row(last).start()
+                for c in range(early, GROUPS):
+                    make_row(c, by_cols)
+                    gram_row(c).start()
             with scope("GIVENEAR"):
                 give_near(part_x, fac_b)
+            with scope("FACOUT"):
+                fac_out[...] += fresh_rate * mul(new, new, dims)
             for c in range(GROUPS):
                 gram_row(c).wait_send()
 

time: 27.5 us -> 26.8 us (0.975)
  the two profiles are of different devices: /device:TPU:12 before, /device:TPU:8 now
where the time goes in v3:
time: 26.8 us; the launch traced here: 26.7 us
  Pallas kernels  26 us (97%)
  between operations  0.64 us (2%)
    pallas_call x1, Pallas kernels, local(): pl.pallas_call(functools.partial(kernel, n_dp, n_mp, blocks, row), out_sh...  24.8 us
    pallas_call x1, Pallas kernels, local(): pl.pallas_call(write_out, out_shape=(jax.ShapeDtypeStruct((bs, bs), F32),...  1.2 us

profile of v3, /device:TPU:8, one launch (start us, length us, event | category | flops | bytes accessed | tf_op | source)
XLA Modules:
  0.0 26.7 jit_solution(12596046005729732382)
XLA Ops:
  0.6 24.8 %refresh.1 = (bf16[16,32,512]{2,1,0:T(8,128)(2,1)S(1)}, f32[512,512]{1,0:T(8,128)S(1)}) custom-call(s32[1,16]{1,0:T(1,128)} %plan.1, bf16[1,512,512]{2,1,0:T(8,128)(2,1)} %bitcast.8, f32[512,512]{1,0:T(8,128)} %bitcast.7, bf16[16,32,512]{2,1,0:T(8,128)(2,1)} %bitcast.9), custom_call_target="tpu_custom_call" | custom-call | tf_op jit(solution)/shard_map/refresh/pallas_call | solution.py:389
  25.5 1.2 %write_out.1 = (f32[512,512]{1,0:T(8,128)}, bf16[16,32,512]{2,1,0:T(8,128)(2,1)}) custom-call(f32[512,512]{1,0:T(8,128)S(1)} %get-tuple-element.6.fac_v, bf16[16,32,512]{2,1,0:T(8,128)(2,1)S(1)} %get-tuple-element.7.fresh_v), custom_call_target="tpu_custom_call" | custom-call | tf_op jit(solution)/shard_map/write_out/pallas_call | solution.py:424

commit v4 on v3

--- a/solution.py
+++ b/solution.py
@@ -28,7 +28,7 @@
     n_dp, n_mp, blocks, row,
     plan, grad, fac, root, fresh, fac_out, plan_s,
     own_g, in_g, fac_v, pieces, full_x, rest, fifth, fac_b, summed, gram_b, out_v,
-    load_sem, grad_send, grad_recv, gram_send, gram_recv, root_send, root_recv, out_send, out_recv, above,
+    load_sem, grad_send, grad_recv, gram_send, gram_recv, root_send, root_recv, out_send, out_recv, ready, above,
 ):
     d = lax.axis_index("dp")
     me = lax.axis_index("mp")
@@ -56,61 +56,31 @@
     partner = d + 1 - 2 * (d % 2)
 
     loads = [
-        pltpu.make_async_copy(grad.at[d // 2], own_g, load_sem.at[0]),
-        pltpu.make_async_copy(root.at[me], pieces.at[me], load_sem.at[1]),
-        pltpu.make_async_copy(fac, fac_v, load_sem.at[2]),
-        pltpu.make_async_copy(plan, plan_s, load_sem.at[3]),
+        pltpu.make_async_copy(root.at[me], pieces.at[me], load_sem.at[0]),
+        pltpu.make_async_copy(fac, fac_v, load_sem.at[1]),
+        pltpu.make_async_copy(plan, plan_s, load_sem.at[2]),
+        pltpu.make_async_copy(grad.at[d // 2], own_g, load_sem.at[3]),
     ]
 
     def signal(sem, dp, mp):
         pl.semaphore_signal(sem, inc=1, device_id=(dp, mp), device_id_type=MESH)
-
-    def by_parity(act):
-        @pl.when(parity == 0)
-        def _():
-            act(True)
-
-        @pl.when(parity == 1)
-        def _():
-            act(False)
-
-    with scope("BARRIER"):
-        barrier = pltpu.get_barrier_semaphore()
-        for i in range(1, n_dp):
-            signal(barrier, (d + i) % n_dp, me)
-        for i in range(1, band):
-            signal(barrier, d, start + (at + i) % band)
-        for k in range(1, levels):
-            @pl.when(level + k < levels)
-            def _():
-                for i in range(band):
-                    signal(barrier, d, start + k * row + (at + i) % band)
-
-        @pl.when(jnp.logical_not(upper_band))
-        def _():
-            for k in range(levels):
-                @pl.when(level + k < levels)
-                def _():
-                    for i in range(band):
-                        signal(barrier, d, start + k * row + band + (at + i) % band)
-
-        for load in loads:
-            load.start()
-        known = n_dp - 1 + band - 1 + level * band
-        pl.semaphore_wait(barrier, jnp.where(upper_band, known + (level + 1) * band, known))
-
-        @pl.when(upper_band)
-        def _():
-            for k in range(levels):
-                @pl.when(level >= k)
-                def _():
-                    signal(above.at[k], d, me - k * row - band)
-                    if k:
-                        signal(above.at[k], d, me - k * row)
 
     def strip(ref, c, by_cols):
         cut = pl.ds(c * wide, wide)
         return ref.at[:, cut] if by_cols else ref.at[cut, :]
+
+    def strips(ref, c, by_cols):
+        cut = pl.ds(c * wide, wide)
+        return ref.at[:, :, cut] if by_cols else ref.at[:, cut, :]
+
+    def by_parity(act):
+        @pl.when(parity == 0)
+        def _():
+            act(True)
+
+        @pl.when(parity == 1)
+        def _():
+            act(False)
 
     def send_grads(by_cols):
         for c in range(GROUPS):
@@ -126,7 +96,65 @@
                         device_id=(to, me), device_id_type=MESH,
                     ).start()
 
-    by_parity(send_grads)
+    with scope("BARRIER"):
+        barrier = pltpu.get_barrier_semaphore()
+        odd_sender = jnp.logical_and(jnp.logical_not(collects), d % 2 == 1)
+
+        @pl.when(collects)
+        def _():
+            for i in range(1, n_dp):
+                signal(barrier, (d + i) % n_dp, me)
+
+        @pl.when(odd_sender)
+        def _():
+            pl.semaphore_wait(barrier, blocks)
+            send_grads(True)
+
+        def greet(first):
+            for i in range(band // 2):
+                t = first + 2 * i + d % 2
+
+                @pl.when(t != me)
+                def _():
+                    signal(barrier, d, t)
+
+        for k in range(levels):
+            @pl.when(level + k < levels)
+            def _():
+                greet(start + k * row)
+
+                @pl.when(jnp.logical_not(upper_band))
+                def _():
+                    greet(start + k * row + band)
+
+        @pl.when(collects)
+        def _():
+            loads[3].start()
+
+        known = blocks - 1 + band - 1 + level * band + jnp.where(upper_band, (level + 1) * band, 0)
+
+        @pl.when(jnp.logical_and(jnp.logical_not(collects), d % 2 == 0))
+        def _():
+            pl.semaphore_wait(barrier, blocks)
+            send_grads(False)
+
+        @pl.when(collects)
+        def _():
+            pl.semaphore_wait(barrier, known)
+            if blocks > 1:
+                by_parity(send_grads)
+            signal(ready, d, me + 1 - 2 * parity)
+
+        @pl.when(jnp.logical_and(upper_band, collects))
+        def _():
+            for k in range(levels):
+                @pl.when(level >= k)
+                def _():
+                    pair = me - at % 2 - k * row
+                    for i in range(2):
+                        signal(above.at[k], d, pair - band + i)
+                        if k:
+                            signal(above.at[k], d, pair + i)
 
     def root_far(t):
         base = side * hb
@@ -191,10 +219,16 @@
                 send_roots((level + k) * row + band, odd)
 
     with scope("ROOTSEND"):
+        @pl.when(jnp.logical_not(collects))
+        def _():
+            pl.semaphore_wait(ready, 1)
+
         each_level(d % 2, True)
+        for load in loads[:3]:
+            load.start()
 
     def take(c, by_cols):
-        wait_bytes(in_g.at[:, :, pl.ds(c * wide, wide)] if by_cols else in_g.at[:, pl.ds(c * wide, wide), :], grad_recv.at[c])
+        wait_bytes(strips(in_g, c, by_cols), grad_recv.at[c])
         total = strip(own_g, c, by_cols)[...].astype(F32)
         for i in range(n_dp - 1):
             total += strip(in_g.at[i], c, by_cols)[...].astype(F32)
@@ -209,16 +243,16 @@
     def gram_row(c):
         part = gram_b.at[pl.ds(c * wide, wide), pl.ds(0, (c + 1) * wide)]
         return pltpu.make_async_remote_copy(
-            src_ref=part, dst_ref=part, send_sem=gram_send.at[c], recv_sem=gram_recv.at[c],
+            src_ref=part, dst_ref=part, send_sem=gram_send, recv_sem=gram_recv.at[c // (GROUPS - 1)],
             device_id=(partner, me), device_id_type=MESH,
         )
 
     early = GROUPS // 2
-    loads[0].wait()
-
     with scope("EARLY"):
         @pl.when(collects)
         def _():
+            loads[3].wait()
+
             def act(by_cols):
                 for c in range(early):
                     take(c, by_cols)
@@ -234,11 +268,11 @@
             each_level(1 - d % 2, False)
 
     with scope("ROOTRECV"):
+        loads[0].wait()
         loads[1].wait()
-        loads[2].wait()
         wait_bytes(pieces.at[pl.ds(0, half - 1 + half * 3 // 8)], root_recv)
 
-    loads[3].wait()
+    loads[2].wait()
     kept = plan_s[0, me] >= n_mp
     x_rate = jnp.where(kept, 1.0, 1.25)
     step = jnp.where(kept, 0.0, 0.25)
@@ -262,56 +296,64 @@
             send_sem=out_send, recv_sem=out_recv, device_id=(d, t), device_id_type=MESH,
         ).start()
 
-    def refine(first, count, base, factor):
+    def refine(first, count, value):
         rows = pl.ds(pl.multiple_of(first * high, high), count * high)
-        refined = base(rows) - mul(fifth[rows, :], factor[...])
-        out_v[pl.ds(first, count)] = refined.reshape(count, high, bs).astype(BF16)
-
-    def give_far(base, factor):
-        for k in range(half // row):
-            refine(away * half + k * row, row, base, factor)
-            for j in range(row):
-                send_out(away * half + k * row + j // 2 * 2 + (j + at) % 2)
-
-    def give_near(base, factor):
-        refine(side * half, half, base, factor)
+        out_v[pl.ds(first, count)] = value(rows).reshape(count, high, bs).astype(BF16)
+
+    def give_far(k, value):
+        to = away * half + k * row
+        refine(to, row, value)
+        for j in range(row):
+            turn = jnp.where(to == 0, j // band, (j // band + 1 + upper_band.astype(jnp.int32)) % 2)
+            send_out(to + turn * band + (at + j) % band)
+
+    def give_near(value):
+        refine(side * half, half, value)
 
         @pl.loop(1, half)
         def _(i):
             send_out(side * half + (me + i) % half)
 
-    def part_x(rows):
-        return x_rate * full_x[rows, :].astype(F32)
+    def with_factor(rows):
+        return x_rate * full_x[rows, :].astype(F32) - mul(fifth[rows, :], fac_b[...])
 
     @pl.when(collects)
     def _():
         def act(by_cols):
             dims = (1, 1) if by_cols else (0, 0)
+            across = (1, 0) if by_cols else (1, 1)
+            back = (1, 1) if by_cols else (1, 0)
             last = GROUPS - 1
+            first_rows = pl.ds(pl.multiple_of(away * hb, hb), row * high)
             with scope("GRADS"):
                 for c in range(early, last):
                     take(c, by_cols)
-                for c in range(early):
+                    make_row(c, by_cols)
+                for c in range(last):
                     gram_row(c).start()
                 cut = pl.ds(0, last * wide)
                 known = summed[:, cut] if by_cols else summed[cut, :]
-                fac_out[...] = keep_rate * fac_v[...] + fresh_rate * mul(known, known, dims)
+                total = keep_rate * fac_v[...] + fresh_rate * mul(known, known, dims)
+                fac_out[...] = total
+                fac_b[...] = total.astype(BF16)
+                rest[first_rows, :] = with_factor(first_rows)
             with scope("GRADLAST"):
                 take(last, by_cols)
                 new = strip(summed, last, by_cols)[...]
+                turned = (fresh_rate * mul(fifth[first_rows, :], new, across)).astype(BF16)
+                give_far(0, lambda rows: rest[rows, :] - mul(turned, new, back))
+            with scope("ROWLAST"):
+                make_row(last, by_cols)
+                gram_row(last).start()
+            with scope("GIVEFAR"):
                 fac_b[...] = (fac_out[...] + fresh_rate * mul(new, new, dims)).astype(BF16)
-            with scope("GIVEFAR"):
-                give_far(part_x, fac_b)
-            with scope("ROWLAST"):
-                for c in range(early, GROUPS):
-                    make_row(c, by_cols)
-                    gram_row(c).start()
+                for k in range(1, half // row):
+                    give_far(k, with_factor)
             with scope("GIVENEAR"):
-                give_near(part_x, fac_b)
+                give_near(with_factor)
             with scope("FACOUT"):
                 fac_out[...] += fresh_rate * mul(new, new, dims)
-            for c in range(GROUPS):
-                gram_row(c).wait_send()
+            wait_bytes(gram_b.at[pl.ds(0, bs * (GROUPS + 1) // (2 * GROUPS))], gram_send)
 
         by_parity(act)
 
@@ -319,17 +361,28 @@
     def _():
         with scope("REST"):
             rest[...] = x_rate * full_x[...].astype(F32) - keep_rate * mul(fifth[...], fac_v[...].astype(BF16))
-        for c in range(GROUPS):
-            with scope("GRAMIN%d" % c):
-                gram_row(c).wait_recv()
-                if c:
-                    rows = pl.ds(c * wide, wide)
-                    before = pl.ds(0, c * wide)
-                    gram_b[before, rows] = gram_b[rows, before].astype(F32).T.astype(BF16)
+        def mirror(c):
+            rows = pl.ds(c * wide, wide)
+            before = pl.ds(0, c * wide)
+            gram_b[before, rows] = gram_b[rows, before].astype(F32).T.astype(BF16)
+
+        last = GROUPS - 1
+        with scope("GRAMIN"):
+            wait_bytes(gram_b.at[pl.ds(0, last * wide), pl.ds(0, bs // 2)], gram_recv.at[0])
+            for c in range(1, last):
+                mirror(c)
+        with scope("GRAMLAST"):
+            gram_row(last).wait_recv()
+            mirror(last)
+
+        def with_gram(rows):
+            return rest[rows, :] - mul(fifth[rows, :], gram_b[...])
+
         with scope("GIVEFAR"):
-            give_far(lambda rows: rest[rows, :], gram_b)
+            for k in range(half // row):
+                give_far(k, with_gram)
         with scope("GIVENEAR"):
-            give_near(lambda rows: rest[rows, :], gram_b)
+            give_near(with_gram)
         with scope("FACOUT"):
             fac_out[...] = keep_rate * fac_v[...] + gram_b[...].astype(F32)
             wait_bytes(in_g.at[pl.ds(0, blocks), pl.ds(0, wide), :], grad_send.at[1])
@@ -359,13 +412,10 @@
 
 
 def write_out(fac_v, fresh_v, fac_out, fresh_out, sem):
-    n = 4
-    copies = []
-    for i in range(n):
-        a = pl.ds(i * (fac_v.shape[0] // n), fac_v.shape[0] // n)
-        b = pl.ds(i * (fresh_v.shape[0] // n), fresh_v.shape[0] // n)
-        copies.append(pltpu.make_async_copy(fac_v.at[a], fac_out.at[a], sem.at[2 * i]))
-        copies.append(pltpu.make_async_copy(fresh_v.at[b], fresh_out.at[b], sem.at[2 * i + 1]))
+    copies = [
+        pltpu.make_async_copy(fac_v, fac_out, sem.at[0]),
+        pltpu.make_async_copy(fresh_v, fresh_out, sem.at[1]),
+    ]
     for copy in copies:
         copy.start()
     for copy in copies:
@@ -410,12 +460,13 @@
             pltpu.SemaphoreType.DMA((4,)),
             pltpu.SemaphoreType.DMA((2,)),
             pltpu.SemaphoreType.DMA((GROUPS,)),
-            pltpu.SemaphoreType.DMA((GROUPS,)),
-            pltpu.SemaphoreType.DMA((GROUPS,)),
+            pltpu.SemaphoreType.DMA,
+            pltpu.SemaphoreType.DMA((2,)),
             pltpu.SemaphoreType.DMA,
             pltpu.SemaphoreType.DMA,
             pltpu.SemaphoreType.DMA,
             pltpu.SemaphoreType.DMA,
+            pltpu.SemaphoreType.REGULAR,
             pltpu.SemaphoreType.REGULAR((n_mp // row,)),
         ],
         compiler_params=pltpu.CompilerParams(collective_id=0, has_side_effects=True),
@@ -429,7 +480,7 @@
         ),
         in_specs=[pl.BlockSpec(memory_space=pl.ANY)] * 2,
         out_specs=(pl.BlockSpec(memory_space=pl.ANY),) * 2,
-        scratch_shapes=[pltpu.SemaphoreType.DMA((8,))],
+        scratch_shapes=[pltpu.SemaphoreType.DMA((2,))],
         compiler_params=pltpu.CompilerParams(vmem_limit_bytes=1 << 20),
         name="write_out",
     )(new_factor, fresh)

time: 26.8 us -> 26.6 us (level)
  no operation moved by 1% of the time
where the time goes in v4:
time: 26.6 us; the launch traced here: 26.5 us
  Pallas kernels  25.8 us (97%)
  between operations  0.64 us (2%)
    pallas_call x1, Pallas kernels, local(): pl.pallas_call(functools.partial(kernel, n_dp, n_mp, blocks, row), out_sh...  24.7 us
    pallas_call x1, Pallas kernels, local(): pl.pallas_call(write_out, out_shape=(jax.ShapeDtypeStruct((bs, bs), F32),...  1.16 us

profile of v4, /device:TPU:8, one launch (start us, length us, event | category | flops | bytes accessed | tf_op | source)
XLA Modules:
  0.0 26.5 jit_solution(1399230612422972718)
XLA Ops:
  0.6 24.7 %refresh.1 = (bf16[16,32,512]{2,1,0:T(8,128)(2,1)S(1)}, f32[512,512]{1,0:T(8,128)S(1)}) custom-call(s32[1,16]{1,0:T(1,128)} %plan.1, bf16[1,512,512]{2,1,0:T(8,128)(2,1)} %bitcast.8, f32[512,512]{1,0:T(8,128)} %bitcast.7, bf16[16,32,512]{2,1,0:T(8,128)(2,1)} %bitcast.9), custom_call_target="tpu_custom_call" | custom-call | tf_op jit(solution)/shard_map/refresh/pallas_call | solution.py:439
  25.3 1.2 %write_out.1 = (f32[512,512]{1,0:T(8,128)}, bf16[16,32,512]{2,1,0:T(8,128)(2,1)}) custom-call(f32[512,512]{1,0:T(8,128)S(1)} %get-tuple-element.6.fac_v, bf16[16,32,512]{2,1,0:T(8,128)(2,1)S(1)} %get-tuple-element.7.fresh_v), custom_call_target="tpu_custom_call" | custom-call | tf_op jit(solution)/shard_map/write_out/pallas_call | solution.py:475

commit v5 on v4

--- a/solution.py
+++ b/solution.py
@@ -27,8 +27,8 @@
 def kernel(
     n_dp, n_mp, blocks, row,
     plan, grad, fac, root, fresh, fac_out, plan_s,
-    own_g, in_g, fac_v, pieces, full_x, rest, fifth, fac_b, summed, gram_b, out_v,
-    load_sem, grad_send, grad_recv, gram_send, gram_recv, root_send, root_recv, out_send, out_recv, ready, above,
+    own_g, in_g, fac_v, pieces, full_x, rest, fifth, fac_b, summed, gram_b, out_v, detour,
+    load_sem, grad_send, grad_recv, gram_send, gram_recv, root_send, root_recv, out_send, out_recv, detour_send, detour_recv, ready, above,
 ):
     d = lax.axis_index("dp")
     me = lax.axis_index("mp")
@@ -296,6 +296,34 @@
             send_sem=out_send, recv_sem=out_recv, device_id=(d, t), device_id_type=MESH,
         ).start()
 
+    middle = levels // 2
+    even = d % 2 == 0
+    hands = jnp.logical_and(jnp.logical_and(collects, even), level == middle)
+    helps = jnp.logical_not(jnp.logical_or(collects, even))
+    first_hop = jnp.logical_and(helps, level == middle)
+    second_hop = jnp.logical_and(helps, level == middle - 1)
+
+    def send_far(t):
+        aside = jnp.logical_and(hands, t == me - row)
+
+        @pl.when(aside)
+        def _():
+            pltpu.make_async_remote_copy(
+                src_ref=out_v.at[t], dst_ref=detour,
+                send_sem=out_send, recv_sem=detour_recv, device_id=(partner, me), device_id_type=MESH,
+            ).start()
+
+        @pl.when(jnp.logical_not(aside))
+        def _():
+            send_out(t)
+
+    def hand_on(to, dst, sem):
+        wait_bytes(detour, detour_recv)
+        pltpu.make_async_remote_copy(
+            src_ref=detour, dst_ref=dst,
+            send_sem=detour_send, recv_sem=sem, device_id=to, device_id_type=MESH,
+        ).start()
+
     def refine(first, count, value):
         rows = pl.ds(pl.multiple_of(first * high, high), count * high)
         out_v[pl.ds(first, count)] = value(rows).reshape(count, high, bs).astype(BF16)
@@ -305,7 +333,7 @@
         refine(to, row, value)
         for j in range(row):
             turn = jnp.where(to == 0, j // band, (j // band + 1 + upper_band.astype(jnp.int32)) % 2)
-            send_out(to + turn * band + (at + j) % band)
+            send_far(to + turn * band + (at + j) % band)
 
     def give_near(value):
         refine(side * half, half, value)
@@ -371,6 +399,10 @@
             wait_bytes(gram_b.at[pl.ds(0, last * wide), pl.ds(0, bs // 2)], gram_recv.at[0])
             for c in range(1, last):
                 mirror(c)
+
+            @pl.when(first_hop)
+            def _():
+                hand_on((d, me - row), detour, detour_recv)
         with scope("GRAMLAST"):
             gram_row(last).wait_recv()
             mirror(last)
@@ -386,6 +418,14 @@
         with scope("FACOUT"):
             fac_out[...] = keep_rate * fac_v[...] + gram_b[...].astype(F32)
             wait_bytes(in_g.at[pl.ds(0, blocks), pl.ds(0, wide), :], grad_send.at[1])
+
+            @pl.when(second_hop)
+            def _():
+                hand_on((partner, me), fresh.at[me + row], out_recv)
+
+            @pl.when(jnp.logical_or(first_hop, second_hop))
+            def _():
+                wait_bytes(detour, detour_send)
 
     with scope("SENDS"):
         own_out = pltpu.make_async_copy(out_v.at[me], fresh.at[me], load_sem.at[0])
@@ -457,11 +497,14 @@
             pltpu.VMEM((bs, bs), BF16),
             pltpu.VMEM((bs, bs), BF16),
             pltpu.VMEM((n_mp, high, bs), BF16),
+            pltpu.VMEM((high, bs), BF16),
             pltpu.SemaphoreType.DMA((4,)),
             pltpu.SemaphoreType.DMA((2,)),
             pltpu.SemaphoreType.DMA((GROUPS,)),
             pltpu.SemaphoreType.DMA,
             pltpu.SemaphoreType.DMA((2,)),
+            pltpu.SemaphoreType.DMA,
+            pltpu.SemaphoreType.DMA,
             pltpu.SemaphoreType.DMA,
             pltpu.SemaphoreType.DMA,
             pltpu.SemaphoreType.DMA,

time: 26.6 us -> 26.3 us (0.989)
  Pallas kernels: 25.8 us -> 25.5 us
    pallas_call x1, Pallas kernels: 24.7 us -> 24.4 us  [local(): pl.pallas_call(functools.partial(kernel, n_dp, n_mp, blocks, row), out_sh...]
where the time goes in v5:
time: 26.3 us; the launch traced here: 26.2 us
  Pallas kernels  25.5 us (97%)
  between operations  0.64 us (2%)
    pallas_call x1, Pallas kernels, local(): pl.pallas_call(functools.partial(kernel, n_dp, n_mp, blocks, row), out_sh...  24.4 us
    pallas_call x1, Pallas kernels, local(): pl.pallas_call(write_out, out_shape=(jax.ShapeDtypeStruct((bs, bs), F32),...  1.16 us

profile of v5, /device:TPU:8, one launch (start us, length us, event | category | flops | bytes accessed | tf_op | source)
XLA Modules:
  0.0 26.2 jit_solution(9027510065622456203)
XLA Ops:
  0.6 24.4 %refresh.1 = (bf16[16,32,512]{2,1,0:T(8,128)(2,1)S(1)}, f32[512,512]{1,0:T(8,128)S(1)}) custom-call(s32[1,16]{1,0:T(1,128)} %plan.1, bf16[1,512,512]{2,1,0:T(8,128)(2,1)} %bitcast.8, f32[512,512]{1,0:T(8,128)} %bitcast.7, bf16[16,32,512]{2,1,0:T(8,128)(2,1)} %bitcast.9), custom_call_target="tpu_custom_call" | custom-call | tf_op jit(solution)/shard_map/refresh/pallas_call | solution.py:479
  25.0 1.2 %write_out.1 = (f32[512,512]{1,0:T(8,128)}, bf16[16,32,512]{2,1,0:T(8,128)(2,1)}) custom-call(f32[512,512]{1,0:T(8,128)S(1)} %get-tuple-element.6.fac_v, bf16[16,32,512]{2,1,0:T(8,128)(2,1)S(1)} %get-tuple-element.7.fresh_v), custom_call_target="tpu_custom_call" | custom-call | tf_op jit(solution)/shard_map/write_out/pallas_call | solution.py:518

commit v6 on v5

--- a/solution.py
+++ b/solution.py
@@ -353,34 +353,52 @@
             back = (1, 1) if by_cols else (1, 0)
             last = GROUPS - 1
             first_rows = pl.ds(pl.multiple_of(away * hb, hb), row * high)
-            with scope("GRADS"):
-                for c in range(early, last):
-                    take(c, by_cols)
-                    make_row(c, by_cols)
-                for c in range(last):
-                    gram_row(c).start()
-                cut = pl.ds(0, last * wide)
-                known = summed[:, cut] if by_cols else summed[cut, :]
-                total = keep_rate * fac_v[...] + fresh_rate * mul(known, known, dims)
-                fac_out[...] = total
-                fac_b[...] = total.astype(BF16)
-                rest[first_rows, :] = with_factor(first_rows)
-            with scope("GRADLAST"):
-                take(last, by_cols)
-                new = strip(summed, last, by_cols)[...]
-                turned = (fresh_rate * mul(fifth[first_rows, :], new, across)).astype(BF16)
-                give_far(0, lambda rows: rest[rows, :] - mul(turned, new, back))
-            with scope("ROWLAST"):
-                make_row(last, by_cols)
-                gram_row(last).start()
+            if by_cols:
+                with scope("GRADS"):
+                    for c in range(early, last):
+                        take(c, by_cols)
+                        make_row(c, by_cols)
+                    for c in range(last):
+                        gram_row(c).start()
+                    known = summed[:, pl.ds(0, last * wide)]
+                    total = keep_rate * fac_v[...] + fresh_rate * mul(known, known, dims)
+                    fac_out[...] = total
+                    fac_b[...] = total.astype(BF16)
+                    rest[first_rows, :] = with_factor(first_rows)
+                with scope("GRADLAST"):
+                    take(last, by_cols)
+                    new = strip(summed, last, by_cols)[...]
+                    turned = (fresh_rate * mul(fifth[first_rows, :], new, across)).astype(BF16)
+                    give_far(0, lambda rows: rest[rows, :] - mul(turned, new, back))
+                with scope("ROWLAST"):
+                    make_row(last, by_cols)
+                    gram_row(last).start()
+                with scope("GIVEFAR"):
+                    fac_b[...] = (fac_out[...] + fresh_rate * mul(new, new, dims)).astype(BF16)
+            else:
+                with scope("GRADS"):
+                    for c in range(early):
+                        gram_row(c).start()
+                    for c in range(early, GROUPS):
+                        take(c, by_cols)
+                    whole = summed[...]
+                    total = keep_rate * fac_v[...] + fresh_rate * mul(whole, whole, dims)
+                    fac_out[...] = total
+                    fac_b[...] = total.astype(BF16)
+                with scope("GRADLAST"):
+                    give_far(0, with_factor)
+                with scope("ROWLAST"):
+                    for c in range(early, GROUPS):
+                        make_row(c, by_cols)
+                        gram_row(c).start()
             with scope("GIVEFAR"):
-                fac_b[...] = (fac_out[...] + fresh_rate * mul(new, new, dims)).astype(BF16)
                 for k in range(1, half // row):
                     give_far(k, with_factor)
             with scope("GIVENEAR"):
                 give_near(with_factor)
-            with scope("FACOUT"):
-                fac_out[...] += fresh_rate * mul(new, new, dims)
+            if by_cols:
+                with scope("FACOUT"):
+                    fac_out[...] += fresh_rate * mul(new, new, dims)
             wait_bytes(gram_b.at[pl.ds(0, bs * (GROUPS + 1) // (2 * GROUPS))], gram_send)
 
         by_parity(act)

time: 26.3 us -> 26.3 us (level)
  no operation moved by 1% of the time
where the time goes in v6:
time: 26.3 us; the launch traced here: 26.1 us
  Pallas kernels  25.5 us (97%)
  between operations  0.64 us (2%)
    pallas_call x1, Pallas kernels, local(): pl.pallas_call(functools.partial(kernel, n_dp, n_mp, blocks, row), out_sh...  24.3 us
    pallas_call x1, Pallas kernels, local(): pl.pallas_call(write_out, out_shape=(jax.ShapeDtypeStruct((bs, bs), F32),...  1.16 us

profile of v6, /device:TPU:8, one launch (start us, length us, event | category | flops | bytes accessed | tf_op | source)
XLA Modules:
  0.0 26.1 jit_solution(16562687715905463525)
XLA Ops:
  0.6 24.3 %refresh.1 = (bf16[16,32,512]{2,1,0:T(8,128)(2,1)S(1)}, f32[512,512]{1,0:T(8,128)S(1)}) custom-call(s32[1,16]{1,0:T(1,128)} %plan.1, bf16[1,512,512]{2,1,0:T(8,128)(2,1)} %bitcast.8, f32[512,512]{1,0:T(8,128)} %bitcast.7, bf16[16,32,512]{2,1,0:T(8,128)(2,1)} %bitcast.9), custom_call_target="tpu_custom_call" | custom-call | tf_op jit(solution)/shard_map/refresh/pallas_call | solution.py:497
  25.0 1.2 %write_out.1 = (f32[512,512]{1,0:T(8,128)}, bf16[16,32,512]{2,1,0:T(8,128)(2,1)}) custom-call(f32[512,512]{1,0:T(8,128)S(1)} %get-tuple-element.6.fac_v, bf16[16,32,512]{2,1,0:T(8,128)(2,1)S(1)} %get-tuple-element.7.fresh_v), custom_call_target="tpu_custom_call" | custom-call | tf_op jit(solution)/shard_map/write_out/pallas_call | solution.py:536

commit v7 on v6

--- a/solution.py
+++ b/solution.py
@@ -333,7 +333,7 @@
         refine(to, row, value)
         for j in range(row):
             turn = jnp.where(to == 0, j // band, (j // band + 1 + upper_band.astype(jnp.int32)) % 2)
-            send_far(to + turn * band + (at + j) % band)
+            send_far(to + turn * band + j % band)
 
     def give_near(value):
         refine(side * half, half, value)

time: 26.3 us -> 26.3 us (level); the launches traced: 26.1 us -> 25.8 us
  Pallas kernels: 25.5 us -> 25.1 us
    pallas_call x1, Pallas kernels: 24.3 us -> 24 us  [local(): pl.pallas_call(functools.partial(kernel, n_dp, n_mp, blocks, row), out_sh...]
where the time goes in v7:
time: 26.3 us; the launch traced here: 25.8 us
  Pallas kernels  25.1 us (95%)
  between operations  0.64 us (2%)
    pallas_call x1, Pallas kernels, local(): pl.pallas_call(functools.partial(kernel, n_dp, n_mp, blocks, row), out_sh...  24 us
    pallas_call x1, Pallas kernels, local(): pl.pallas_call(write_out, out_shape=(jax.ShapeDtypeStruct((bs, bs), F32),...  1.16 us

profile of v7, /device:TPU:8, one launch (start us, length us, event | category | flops | bytes accessed | tf_op | source)
XLA Modules:
  0.0 25.8 jit_solution(11178738025985295801)
XLA Ops:
  0.6 24.0 %refresh.1 = (bf16[16,32,512]{2,1,0:T(8,128)(2,1)S(1)}, f32[512,512]{1,0:T(8,128)S(1)}) custom-call(s32[1,16]{1,0:T(1,128)} %plan.1, bf16[1,512,512]{2,1,0:T(8,128)(2,1)} %bitcast.8, f32[512,512]{1,0:T(8,128)} %bitcast.7, bf16[16,32,512]{2,1,0:T(8,128)(2,1)} %bitcast.9), custom_call_target="tpu_custom_call" | custom-call | tf_op jit(solution)/shard_map/refresh/pallas_call | solution.py:497
  24.6 1.2 %write_out.1 = (f32[512,512]{1,0:T(8,128)}, bf16[16,32,512]{2,1,0:T(8,128)(2,1)}) custom-call(f32[512,512]{1,0:T(8,128)S(1)} %get-tuple-element.6.fac_v, bf16[16,32,512]{2,1,0:T(8,128)(2,1)S(1)} %get-tuple-element.7.fresh_v), custom_call_target="tpu_custom_call" | custom-call | tf_op jit(solution)/shard_map/write_out/pallas_call | solution.py:536

commit v8 on v7

--- a/solution.py
+++ b/solution.py
@@ -333,7 +333,7 @@
         refine(to, row, value)
         for j in range(row):
             turn = jnp.where(to == 0, j // band, (j // band + 1 + upper_band.astype(jnp.int32)) % 2)
-            send_far(to + turn * band + j % band)
+            send_far(to + turn * band + (j + d) % band)
 
     def give_near(value):
         refine(side * half, half, value)

time: 26.3 us -> 26.3 us (level)
  no operation moved by 1% of the time
where the time goes in v8:
time: 26.3 us; the launch traced here: 25.8 us
  Pallas kernels  25.1 us (95%)
  between operations  0.64 us (2%)
    pallas_call x1, Pallas kernels, local(): pl.pallas_call(functools.partial(kernel, n_dp, n_mp, blocks, row), out_sh...  24 us
    pallas_call x1, Pallas kernels, local(): pl.pallas_call(write_out, out_shape=(jax.ShapeDtypeStruct((bs, bs), F32),...  1.16 us

profile of v8, /device:TPU:8, one launch (start us, length us, event | category | flops | bytes accessed | tf_op | source)
XLA Modules:
  0.0 25.8 jit_solution(146530620917841712)
XLA Ops:
  0.6 24.0 %refresh.1 = (bf16[16,32,512]{2,1,0:T(8,128)(2,1)S(1)}, f32[512,512]{1,0:T(8,128)S(1)}) custom-call(s32[1,16]{1,0:T(1,128)} %plan.1, bf16[1,512,512]{2,1,0:T(8,128)(2,1)} %bitcast.8, f32[512,512]{1,0:T(8,128)} %bitcast.7, bf16[16,32,512]{2,1,0:T(8,128)(2,1)} %bitcast.9), custom_call_target="tpu_custom_call" | custom-call | tf_op jit(solution)/shard_map/refresh/pallas_call | solution.py:497
  24.6 1.2 %write_out.1 = (f32[512,512]{1,0:T(8,128)}, bf16[16,32,512]{2,1,0:T(8,128)(2,1)}) custom-call(f32[512,512]{1,0:T(8,128)S(1)} %get-tuple-element.6.fac_v, bf16[16,32,512]{2,1,0:T(8,128)(2,1)S(1)} %get-tuple-element.7.fresh_v), custom_call_target="tpu_custom_call" | custom-call | tf_op jit(solution)/shard_map/write_out/pallas_call | solution.py:536
